TPU v7x, 32 devices: a whole 2x2x4 slice. The times are simulated.
32 devices in a mesh: section: 16 (over z, x, core), dp: 2 (over y).
Axes of the slice: x: 2, y: 2, z: 4, core: 2. Of those that a mesh axis runs over, the one named last changes fastest.
Arguments:
- cotangent: bfloat16 [128, 8192], P('dp'), may hold values from -96 to 96
- lengths: int32 [4], P('dp'), may hold values from 1 to 32, as said below
- example_ids: int32 [128], P('dp'), may hold values from -1 to 3, as said below
- layer_inputs: bfloat16 [128, 32768], P('dp', 'section'), may hold values from -6 to 6
- preacts: bfloat16 [128, 32768], P('dp', 'section'), may hold values from -6 to 6
- weights: bfloat16 [32768, 8192], P('section', 'dp'), may hold values from -0.0625 to 0.0625
- query_left: bfloat16 [32768, 256], P('section'), may hold values from -0.0625 to 0.0625
- query_right: bfloat16 [32768, 256], P('section'), may hold values from -0.0625 to 0.0625
Outputs:
- input_grads: bfloat16 [128, 32768], P('dp', 'section')
- scores: float32 [4, 16], P('dp')
Inputs may be any that keep to these rules, and one draw needn't show every extreme that they name: In each aligned block of 2 sequences one length is exactly 32; the lengths of a block sum to at most 64. `example_ids`: rows n * 64 to (n + 1) * 64 - 1 hold sequences n * 2 to (n + 1) * 2 - 1 in order from the block's first row, each on as many consecutive rows as its length; the block's remaining rows hold -1.
All inputs are finite; a program needn't handle non-finite values.
Results may differ from a plain program's by a relative error of at most 0.0066.
Values may be sent and summed in bfloat16 or wider, within the bound.
No kernel may reach another device: no remote copies, remote signals or barrier semaphores. Data moves between devices by JAX's collectives and lax.ppermute only.
A program may use at most 64 MiB of HBM per device.

v0:
```python
import jax
import jax.numpy as jnp
from jax import lax
from jax.sharding import PartitionSpec as P

LAYERS = 4
QUERIES = 16
RANK = 16
ROWS = 32


def from_partner(value, axis, distance):
    mask = 2**distance
    pairs = [(source, source ^ mask) for source in range(lax.axis_size(axis))]
    return lax.ppermute(value, axis, pairs)


def from_behind(value, axis, steps):
    count = lax.axis_size(axis)
    first, last = (max(0, -steps), min(count, count - steps))
    return lax.ppermute(value, axis, [(source, source + steps) for source in range(first, last)])


def silu_slope(preact):
    sigmoid_value = jax.nn.sigmoid(preact)
    return sigmoid_value * (1.0 + preact * (1.0 - sigmoid_value))


def per_device(
    cotangent, lengths, example_ids, layer_inputs, preacts, weights, query_left, query_right
):
    per_section = lax.axis_size("section") // LAYERS
    level_count = per_section.bit_length() - 1
    position = lax.axis_index("section")
    section_index = position // per_section
    column_block = position % per_section
    group_index = lax.axis_index("dp")
    token_count = cotangent.shape[0]
    block_cols = layer_inputs.shape[1]
    seq_count = lengths.shape[0]
    micro_count = token_count // ROWS
    step_count = LAYERS + micro_count - 1
    seq_slots = group_index * seq_count + jnp.arange(seq_count, dtype=jnp.int32)
    member = (example_ids[:, None] == seq_slots[None, :]).astype(jnp.float32)
    token_len = jnp.dot(member, lengths.astype(jnp.float32), precision=lax.Precision.HIGHEST)
    token_scale = jnp.where(example_ids >= 0, 1.0 / jnp.maximum(token_len, 1.0), 0.0)
    top_columns = lax.dynamic_slice_in_dim(cotangent, column_block * block_cols, block_cols, 1)
    top_grad = (top_columns.astype(jnp.float32) * token_scale[:, None]).astype(jnp.bfloat16)
    right_full = query_right
    for level_bit in range(level_count):
        partner = from_partner(right_full, "section", level_bit)
        upper_half = column_block >> level_bit & 1
        right_full = jnp.where(
            upper_half == 1,
            jnp.concatenate([partner, right_full], 0),
            jnp.concatenate([right_full, partner], 0),
        )

    def gather_gate(gate_grad):
        combined = gate_grad
        for level_bit in range(level_count):
            partner = from_partner(combined, "section", level_bit)
            upper_half = column_block >> level_bit & 1
            combined = jnp.where(
                upper_half == 1,
                jnp.concatenate([partner, combined], 1),
                jnp.concatenate([combined, partner], 1),
            )
        return combined

    def score_terms(gate_full, input_rows, id_rows):
        left_part = jnp.dot(input_rows, query_left, preferred_element_type=jnp.float32)
        right_part = jnp.dot(gate_full, right_full, preferred_element_type=jnp.float32)
        per_token = jnp.sum((left_part * right_part).reshape(ROWS, QUERIES, RANK), axis=2)
        block_member = (id_rows[:, None] == seq_slots[None, :]).astype(jnp.float32)
        return jnp.dot(block_member.T, per_token, precision=lax.Precision.HIGHEST)

    def advance(clock_tick, loop_state):
        outgoing, grad_store, totals = loop_state
        arrived = from_behind(outgoing, "section", -per_section)
        micro_index = clock_tick - (LAYERS - 1 - section_index)
        in_range = (micro_index >= 0) & (micro_index < micro_count)
        row_start = jnp.clip(micro_index, 0, micro_count - 1) * ROWS
        top_rows = lax.dynamic_slice_in_dim(top_grad, row_start, ROWS, 0)
        grad_out = jnp.where(section_index == LAYERS - 1, top_rows, arrived)
        preact = lax.dynamic_slice_in_dim(preacts, row_start, ROWS, 0).astype(jnp.float32)
        gate_grad = (silu_slope(preact) * grad_out.astype(jnp.float32)).astype(jnp.bfloat16)
        gate_full = gather_gate(gate_grad)
        input_rows = lax.dynamic_slice_in_dim(layer_inputs, row_start, ROWS, 0)
        id_rows = lax.dynamic_slice_in_dim(example_ids, row_start, ROWS, 0)
        by_group = lax.all_to_all(gate_full, "dp", split_axis=1, concat_axis=0, tiled=True)
        backward_sum = lax.psum_scatter(
            lax.dot_general(
                by_group, weights, (((1,), (1,)), ((), ())), preferred_element_type=jnp.float32
            ),
            "dp",
            scatter_dimension=0,
            tiled=True,
        )
        increment = score_terms(gate_full, input_rows, id_rows)
        in_grad = (grad_out.astype(jnp.float32) + backward_sum).astype(jnp.bfloat16)
        updated = lax.dynamic_update_slice_in_dim(grad_store, in_grad, row_start, 0)
        grad_store = jnp.where(in_range, updated, grad_store)
        increment = jnp.where(in_range, increment, 0.0)
        totals = totals + lax.psum(increment, "section")
        return (in_grad, grad_store, totals)

    initial = (
        jnp.zeros((ROWS, block_cols), jnp.bfloat16),
        jnp.zeros((token_count, block_cols), jnp.bfloat16),
        jnp.zeros((seq_count, QUERIES), jnp.float32),
    )
    outgoing, grad_store, totals = lax.fori_loop(0, step_count, advance, initial)
    return (grad_store, totals)


def solution(mesh):
    placed = (
        P("dp", None),
        P("dp"),
        P("dp"),
        P("dp", "section"),
        P("dp", "section"),
        P("section", "dp"),
        P("section", None),
        P("section", None),
    )
    return jax.shard_map(
        per_device,
        mesh=mesh,
        in_specs=placed,
        out_specs=(P("dp", "section"), P("dp", None)),
        check_vma=False,
    )
```

profile of v0, /device:TPU:0, one launch (start us, length us, event | category | flops | bytes accessed | tf_op | source)
XLA Modules:
  0.0 443.8 jit_solution(1843948315144772857)
XLA Ops:
  10.2 3.4 maximum_select_fusion.6
  17.8 44.9 %collective-permute-done.4 = bf16[4096,256]{1,0:T(8,128)(2,1)} collective-permute-done((bf16[4096,256]{1,0:T(8,128)(2,1)}, bf16[4096,256]{1,0:T(8,128)(2,1)}, u32[]{:S(2)}, u32[]{:S(2)}) %collective-permute-start.4) | collective-permute-done | bytes 2097184 | tf_op jit(solution)/shard_map/ppermute | solution.py:15
  62.7 5.5 %maximum_select_fusion.5 = bf16[8192,256]{1,0:T(8,128)(2,1)} fusion(bf16[4096,256]{1,0:T(8,128)(2,1)} %maximum_select_fusion.6, bf16[4096,256]{1,0:T(8,128)(2,1)} %collective-permute-done.4, pred[]{:T(512)} %eq.87), kind=kLoop, calls=%fused_computation.37 | loop fusion | flops 18874368 | bytes 8388609 | tf_op jit(solution)/shard_map/jit(_where)/select_n | solution.py:53
  68.3 368.3 %while.20 = (s32[]{:T(128)}, bf16[32,2048]{1,0:T(8,128)(2,1)S(1)}, bf16[64,2048]{1,0:T(8,128)(2,1)S(1)}, f32[2,16]{1,0:T(2,128)S(1)}, pred[]{:T(512)}, /*index=5...) while((s32[]{:T(128)}, bf16[32,2048]{1,0:T(8,128)(2,1)S(1)}, ...), condition=%wide.region_4.5_spmd.clone, body=%wide.region_0.4_spmd.clone.sunk | while | flops 1248227072 | bytes 33232504 | solution.py:113
  69.7 5.5 %collective-permute-done = bf16[32,2048]{1,0:T(8,128)(2,1)S(1)} collective-permute-done((bf16[32,2048]{1,0:T(8,128)(2,1)S(1)}, bf16[32,2048]{1,0:T(8,128)(2,1)S(1)}, u32[]{:S(2)}, u32[]{:S(2)}) %collective-permute-start) | collective-permute-done | bytes 131104 | tf_op jit(solution)/shard_map/while/body/eval_jaxpr/ppermute | solution.py:21
  78.7 6.5 %collective-permute-done.2 = bf16[32,4096]{1,0:T(8,128)(2,1)S(1)} collective-permute-done((bf16[32,4096]{1,0:T(8,128)(2,1)S(1)}, bf16[32,4096]{1,0:T(8,128)(2,1)S(1)}, u32[]{:S(2)}, u32[]{:S(2)}) %collective-permute-start.2) | collective-permute-done | bytes 262176 | tf_op jit(solution)/shard_map/while/body/eval_jaxpr/ppermute | solution.py:15
  85.3 10.3 %all_to_all.38 = bf16[32,2,4096]{2,0,1:T(8,128)(2,1)S(1)} all-to-all(bf16[32,2,4096]{2,0,1:T(8,128)(2,1)S(1)} %maximum_select_fusion.14), channel_id=1, replica_groups=mesh['section'=16,'dp'=2] {'dp'}, dimensions={1} | all-to-all | bytes 1048576 | tf_op jit(solution)/shard_map/while/body/eval_jaxpr/all_to_all | solution.py:91
  95.6 11.8 %fusion.50 = f32[64,2048]{1,0:T(8,128)} fusion(bf16[64,4096]{1,0:T(8,128)(2,1)S(1)} %bitcast.44, bf16[2048,4096]{1,0:T(8,128)(2,1)} %get-tuple-element.579), kind=kOutput, calls=%fused_computation.49.clone.1 | convolution fusion | flops 1073741824 | bytes 17825792 | tf_op jit(solution)/shard_map/while/body/eval_jaxpr/dot_general | solution.py:93
  111.1 30.1 %psum.15 = f32[2,16]{1,0:T(2,128)S(1)} all-reduce(f32[2,16]{1,0:T(2,128)S(1)} %convolution_select_fusion.2), channel_id=1, replica_groups=mesh['section'=16,'dp'=2] {'section'}, use_global_device_ids=true, to_apply=%region_3.3 | all-reduce | flops 32 | bytes 256 | tf_op jit(solution)/shard_map/while/body/eval_jaxpr/psum | solution.py:105
  143.6 5.5 %collective-permute-done = bf16[32,2048]{1,0:T(8,128)(2,1)S(1)} collective-permute-done((bf16[32,2048]{1,0:T(8,128)(2,1)S(1)}, bf16[32,2048]{1,0:T(8,128)(2,1)S(1)}, u32[]{:S(2)}, u32[]{:S(2)}) %collective-permute-start) | collective-permute-done | bytes 131104 | tf_op jit(solution)/shard_map/while/body/eval_jaxpr/ppermute | solution.py:21
  151.0 8.3 %collective-permute-done.2 = bf16[32,4096]{1,0:T(8,128)(2,1)S(1)} collective-permute-done((bf16[32,4096]{1,0:T(8,128)(2,1)S(1)}, bf16[32,4096]{1,0:T(8,128)(2,1)S(1)}, u32[]{:S(2)}, u32[]{:S(2)}) %collective-permute-start.2) | collective-permute-done | bytes 262176 | tf_op jit(solution)/shard_map/while/body/eval_jaxpr/ppermute | solution.py:15
  159.3 10.1 %all_to_all.38 = bf16[32,2,4096]{2,0,1:T(8,128)(2,1)S(1)} all-to-all(bf16[32,2,4096]{2,0,1:T(8,128)(2,1)S(1)} %maximum_select_fusion.14), channel_id=1, replica_groups=mesh['section'=16,'dp'=2] {'dp'}, dimensions={1} | all-to-all | bytes 1048576 | tf_op jit(solution)/shard_map/while/body/eval_jaxpr/all_to_all | solution.py:91
  169.4 11.8 %fusion.50 = f32[64,2048]{1,0:T(8,128)} fusion(bf16[64,4096]{1,0:T(8,128)(2,1)S(1)} %bitcast.44, bf16[2048,4096]{1,0:T(8,128)(2,1)} %get-tuple-element.579), kind=kOutput, calls=%fused_computation.49.clone.1 | convolution fusion | flops 1073741824 | bytes 17825792 | tf_op jit(solution)/shard_map/while/body/eval_jaxpr/dot_general | solution.py:93
  181.6 3.0 convolution_multiply_fusion.2
  185.0 29.5 %psum.15 = f32[2,16]{1,0:T(2,128)S(1)} all-reduce(f32[2,16]{1,0:T(2,128)S(1)} %convolution_select_fusion.2), channel_id=1, replica_groups=mesh['section'=16,'dp'=2] {'section'}, use_global_device_ids=true, to_apply=%region_3.3 | all-reduce | flops 32 | bytes 256 | tf_op jit(solution)/shard_map/while/body/eval_jaxpr/psum | solution.py:105
  216.9 5.9 %collective-permute-done = bf16[32,2048]{1,0:T(8,128)(2,1)S(1)} collective-permute-done((bf16[32,2048]{1,0:T(8,128)(2,1)S(1)}, bf16[32,2048]{1,0:T(8,128)(2,1)S(1)}, u32[]{:S(2)}, u32[]{:S(2)}) %collective-permute-start) | collective-permute-done | bytes 131104 | tf_op jit(solution)/shard_map/while/body/eval_jaxpr/ppermute | solution.py:21
  224.6 8.3 %collective-permute-done.2 = bf16[32,4096]{1,0:T(8,128)(2,1)S(1)} collective-permute-done((bf16[32,4096]{1,0:T(8,128)(2,1)S(1)}, bf16[32,4096]{1,0:T(8,128)(2,1)S(1)}, u32[]{:S(2)}, u32[]{:S(2)}) %collective-permute-start.2) | collective-permute-done | bytes 262176 | tf_op jit(solution)/shard_map/while/body/eval_jaxpr/ppermute | solution.py:15
  233.0 10.1 %all_to_all.38 = bf16[32,2,4096]{2,0,1:T(8,128)(2,1)S(1)} all-to-all(bf16[32,2,4096]{2,0,1:T(8,128)(2,1)S(1)} %maximum_select_fusion.14), channel_id=1, replica_groups=mesh['section'=16,'dp'=2] {'dp'}, dimensions={1} | all-to-all | bytes 1048576 | tf_op jit(solution)/shard_map/while/body/eval_jaxpr/all_to_all | solution.py:91
  243.1 11.8 %fusion.50 = f32[64,2048]{1,0:T(8,128)} fusion(bf16[64,4096]{1,0:T(8,128)(2,1)S(1)} %bitcast.44, bf16[2048,4096]{1,0:T(8,128)(2,1)} %get-tuple-element.579), kind=kOutput, calls=%fused_computation.49.clone.1 | convolution fusion | flops 1073741824 | bytes 17825792 | tf_op jit(solution)/shard_map/while/body/eval_jaxpr/dot_general | solution.py:93
  258.7 29.5 %psum.15 = f32[2,16]{1,0:T(2,128)S(1)} all-reduce(f32[2,16]{1,0:T(2,128)S(1)} %convolution_select_fusion.2), channel_id=1, replica_groups=mesh['section'=16,'dp'=2] {'section'}, use_global_device_ids=true, to_apply=%region_3.3 | all-reduce | flops 32 | bytes 256 | tf_op jit(solution)/shard_map/while/body/eval_jaxpr/psum | solution.py:105
  290.6 5.9 %collective-permute-done = bf16[32,2048]{1,0:T(8,128)(2,1)S(1)} collective-permute-done((bf16[32,2048]{1,0:T(8,128)(2,1)S(1)}, bf16[32,2048]{1,0:T(8,128)(2,1)S(1)}, u32[]{:S(2)}, u32[]{:S(2)}) %collective-permute-start) | collective-permute-done | bytes 131104 | tf_op jit(solution)/shard_map/while/body/eval_jaxpr/ppermute | solution.py:21
  298.3 8.3 %collective-permute-done.2 = bf16[32,4096]{1,0:T(8,128)(2,1)S(1)} collective-permute-done((bf16[32,4096]{1,0:T(8,128)(2,1)S(1)}, bf16[32,4096]{1,0:T(8,128)(2,1)S(1)}, u32[]{:S(2)}, u32[]{:S(2)}) %collective-permute-start.2) | collective-permute-done | bytes 262176 | tf_op jit(solution)/shard_map/while/body/eval_jaxpr/ppermute | solution.py:15
  306.7 10.1 %all_to_all.38 = bf16[32,2,4096]{2,0,1:T(8,128)(2,1)S(1)} all-to-all(bf16[32,2,4096]{2,0,1:T(8,128)(2,1)S(1)} %maximum_select_fusion.14), channel_id=1, replica_groups=mesh['section'=16,'dp'=2] {'dp'}, dimensions={1} | all-to-all | bytes 1048576 | tf_op jit(solution)/shard_map/while/body/eval_jaxpr/all_to_all | solution.py:91
  316.8 11.8 %fusion.50 = f32[64,2048]{1,0:T(8,128)} fusion(bf16[64,4096]{1,0:T(8,128)(2,1)S(1)} %bitcast.44, bf16[2048,4096]{1,0:T(8,128)(2,1)} %get-tuple-element.579), kind=kOutput, calls=%fused_computation.49.clone.1 | convolution fusion | flops 1073741824 | bytes 17825792 | tf_op jit(solution)/shard_map/while/body/eval_jaxpr/dot_general | solution.py:93
  329.0 3.0 convolution_multiply_fusion.2
  332.4 29.5 %psum.15 = f32[2,16]{1,0:T(2,128)S(1)} all-reduce(f32[2,16]{1,0:T(2,128)S(1)} %convolution_select_fusion.2), channel_id=1, replica_groups=mesh['section'=16,'dp'=2] {'section'}, use_global_device_ids=true, to_apply=%region_3.3 | all-reduce | flops 32 | bytes 256 | tf_op jit(solution)/shard_map/while/body/eval_jaxpr/psum | solution.py:105
  364.3 5.9 %collective-permute-done = bf16[32,2048]{1,0:T(8,128)(2,1)S(1)} collective-permute-done((bf16[32,2048]{1,0:T(8,128)(2,1)S(1)}, bf16[32,2048]{1,0:T(8,128)(2,1)S(1)}, u32[]{:S(2)}, u32[]{:S(2)}) %collective-permute-start) | collective-permute-done | bytes 131104 | tf_op jit(solution)/shard_map/while/body/eval_jaxpr/ppermute | solution.py:21
  372.0 8.3 %collective-permute-done.2 = bf16[32,4096]{1,0:T(8,128)(2,1)S(1)} collective-permute-done((bf16[32,4096]{1,0:T(8,128)(2,1)S(1)}, bf16[32,4096]{1,0:T(8,128)(2,1)S(1)}, u32[]{:S(2)}, u32[]{:S(2)}) %collective-permute-start.2) | collective-permute-done | bytes 262176 | tf_op jit(solution)/shard_map/while/body/eval_jaxpr/ppermute | solution.py:15
  380.4 10.1 %all_to_all.38 = bf16[32,2,4096]{2,0,1:T(8,128)(2,1)S(1)} all-to-all(bf16[32,2,4096]{2,0,1:T(8,128)(2,1)S(1)} %maximum_select_fusion.14), channel_id=1, replica_groups=mesh['section'=16,'dp'=2] {'dp'}, dimensions={1} | all-to-all | bytes 1048576 | tf_op jit(solution)/shard_map/while/body/eval_jaxpr/all_to_all | solution.py:91
  390.5 11.8 %fusion.50 = f32[64,2048]{1,0:T(8,128)} fusion(bf16[64,4096]{1,0:T(8,128)(2,1)S(1)} %bitcast.44, bf16[2048,4096]{1,0:T(8,128)(2,1)} %get-tuple-element.579), kind=kOutput, calls=%fused_computation.49.clone.1 | convolution fusion | flops 1073741824 | bytes 17825792 | tf_op jit(solution)/shard_map/while/body/eval_jaxpr/dot_general | solution.py:93
  402.7 3.0 convolution_multiply_fusion.2
  406.0 29.5 %psum.15 = f32[2,16]{1,0:T(2,128)S(1)} all-reduce(f32[2,16]{1,0:T(2,128)S(1)} %convolution_select_fusion.2), channel_id=1, replica_groups=mesh['section'=16,'dp'=2] {'section'}, use_global_device_ids=true, to_apply=%region_3.3 | all-reduce | flops 32 | bytes 256 | tf_op jit(solution)/shard_map/while/body/eval_jaxpr/psum | solution.py:105
  (125 shorter events, 40.4 us)
Async XLA Ops:
  7.2 9.3 %copy-start.5 = (s32[2]{0:T(128)S(1)}, s32[2]{0:T(128)}, u32[]{:S(2)}) copy-start(s32[2]{0:T(128)} %param.11) | copy-start | bytes 28
  7.2 9.3 %copy-start.6 = (s32[64]{0:T(128)S(1)}, s32[64]{0:T(128)}, u32[]{:S(2)}) copy-start(s32[64]{0:T(128)} %param.12) | copy-start | bytes 772
  7.2 3.1 collective-permute-start.3
  13.6 49.1 %collective-permute-start.4 = (bf16[4096,256]{1,0:T(8,128)(2,1)}, bf16[4096,256]{1,0:T(8,128)(2,1)}, u32[]{:S(2)}, u32[]{:S(2)}) collective-permute-start(bf16[4096,256]{1,0:T(8,128)(2,1)} %maximum_select_fusion.6), channel_id=1, source_target_pairs={{0,4},{2,6},{4,0},{6,2},{8,12},{10,14},{12,8},{14,10},{16,20},{18,... | collective-permute-start | bytes 6291464 | tf_op jit(solution)/shard_map/ppermute | solution.py:15
  17.8 50.5 %copy-start = (bf16[2048,256]{1,0:T(8,128)(2,1)S(1)}, bf16[2048,256]{1,0:T(8,128)(2,1)}, u32[]{:S(2)}) copy-start(bf16[2048,256]{1,0:T(8,128)(2,1)} %param.16) | copy-start | bytes 3145732
  17.8 50.5 %copy-start.2 = (bf16[64,2048]{1,0:T(8,128)(2,1)S(1)}, bf16[64,2048]{1,0:T(8,128)(2,1)}, u32[]{:S(2)}) copy-start(bf16[64,2048]{1,0:T(8,128)(2,1)} %param.13) | copy-start | bytes 786436
  17.8 50.5 %copy-start.3 = (bf16[64,2048]{1,0:T(8,128)(2,1)S(1)}, bf16[64,2048]{1,0:T(8,128)(2,1)}, u32[]{:S(2)}) copy-start(bf16[64,2048]{1,0:T(8,128)(2,1)} %param.14) | copy-start | bytes 786436
  68.3 72.9 %reduce-scatter.2.cloned.1.call-start = ((), (), s32[]{:S(2)}) async-start(), calls=%async_computation.2 | async-start | bytes 786432 | tf_op jit(solution)/shard_map/while/body/eval_jaxpr/reduce_scatter | solution.py:92
  68.4 6.9 %collective-permute-start = (bf16[32,2048]{1,0:T(8,128)(2,1)S(1)}, bf16[32,2048]{1,0:T(8,128)(2,1)S(1)}, u32[]{:S(2)}, u32[]{:S(2)}) collective-permute-start(bf16[32,2048]{1,0:T(8,128)(2,1)S(1)} %broadcast_select_fusion.2), channel_id=1, source_target_pairs={{8,0},{10,2},{12,4},{14,6},{16,8},{18,10},{20,12},{22,14},{24,16},... | collective-permute-start | bytes 393224 | tf_op jit(solution)/shard_map/while/body/eval_jaxpr/ppermute | solution.py:21
  75.3 1.4 collective-permute-start.1
  76.8 8.4 %collective-permute-start.2 = (bf16[32,4096]{1,0:T(8,128)(2,1)S(1)}, bf16[32,4096]{1,0:T(8,128)(2,1)S(1)}, u32[]{:S(2)}, u32[]{:S(2)}) collective-permute-start(bf16[32,4096]{1,0:T(8,128)(2,1)S(1)} %maximum_select_fusion.13), channel_id=1, source_target_pairs={{0,4},{2,6},{4,0},{6,2},{8,12},{10,14},{12,8},{14,10},{16,20},{18,... | collective-permute-start | bytes 786440 | tf_op jit(solution)/shard_map/while/body/eval_jaxpr/ppermute | solution.py:15
  142.2 72.2 %reduce-scatter.2.cloned.1.call-start = ((), (), s32[]{:S(2)}) async-start(), calls=%async_computation.2 | async-start | bytes 786432 | tf_op jit(solution)/shard_map/while/body/eval_jaxpr/reduce_scatter | solution.py:92
  142.3 6.9 %collective-permute-start = (bf16[32,2048]{1,0:T(8,128)(2,1)S(1)}, bf16[32,2048]{1,0:T(8,128)(2,1)S(1)}, u32[]{:S(2)}, u32[]{:S(2)}) collective-permute-start(bf16[32,2048]{1,0:T(8,128)(2,1)S(1)} %broadcast_select_fusion.2), channel_id=1, source_target_pairs={{8,0},{10,2},{12,4},{14,6},{16,8},{18,10},{20,12},{22,14},{24,16},... | collective-permute-start | bytes 393224 | tf_op jit(solution)/shard_map/while/body/eval_jaxpr/ppermute | solution.py:21
  149.3 1.4 collective-permute-start.1
  150.8 8.4 %collective-permute-start.2 = (bf16[32,4096]{1,0:T(8,128)(2,1)S(1)}, bf16[32,4096]{1,0:T(8,128)(2,1)S(1)}, u32[]{:S(2)}, u32[]{:S(2)}) collective-permute-start(bf16[32,4096]{1,0:T(8,128)(2,1)S(1)} %maximum_select_fusion.13), channel_id=1, source_target_pairs={{0,4},{2,6},{4,0},{6,2},{8,12},{10,14},{12,8},{14,10},{16,20},{18,... | collective-permute-start | bytes 786440 | tf_op jit(solution)/shard_map/while/body/eval_jaxpr/ppermute | solution.py:15
  215.5 72.6 %reduce-scatter.2.cloned.1.call-start = ((), (), s32[]{:S(2)}) async-start(), calls=%async_computation.2 | async-start | bytes 786432 | tf_op jit(solution)/shard_map/while/body/eval_jaxpr/reduce_scatter | solution.py:92
  215.6 7.3 %collective-permute-start = (bf16[32,2048]{1,0:T(8,128)(2,1)S(1)}, bf16[32,2048]{1,0:T(8,128)(2,1)S(1)}, u32[]{:S(2)}, u32[]{:S(2)}) collective-permute-start(bf16[32,2048]{1,0:T(8,128)(2,1)S(1)} %broadcast_select_fusion.2), channel_id=1, source_target_pairs={{8,0},{10,2},{12,4},{14,6},{16,8},{18,10},{20,12},{22,14},{24,16},... | collective-permute-start | bytes 393224 | tf_op jit(solution)/shard_map/while/body/eval_jaxpr/ppermute | solution.py:21
  223.0 1.4 collective-permute-start.1
  224.5 8.4 %collective-permute-start.2 = (bf16[32,4096]{1,0:T(8,128)(2,1)S(1)}, bf16[32,4096]{1,0:T(8,128)(2,1)S(1)}, u32[]{:S(2)}, u32[]{:S(2)}) collective-permute-start(bf16[32,4096]{1,0:T(8,128)(2,1)S(1)} %maximum_select_fusion.13), channel_id=1, source_target_pairs={{0,4},{2,6},{4,0},{6,2},{8,12},{10,14},{12,8},{14,10},{16,20},{18,... | collective-permute-start | bytes 786440 | tf_op jit(solution)/shard_map/while/body/eval_jaxpr/ppermute | solution.py:15
  289.2 72.6 %reduce-scatter.2.cloned.1.call-start = ((), (), s32[]{:S(2)}) async-start(), calls=%async_computation.2 | async-start | bytes 786432 | tf_op jit(solution)/shard_map/while/body/eval_jaxpr/reduce_scatter | solution.py:92
  289.3 7.3 %collective-permute-start = (bf16[32,2048]{1,0:T(8,128)(2,1)S(1)}, bf16[32,2048]{1,0:T(8,128)(2,1)S(1)}, u32[]{:S(2)}, u32[]{:S(2)}) collective-permute-start(bf16[32,2048]{1,0:T(8,128)(2,1)S(1)} %broadcast_select_fusion.2), channel_id=1, source_target_pairs={{8,0},{10,2},{12,4},{14,6},{16,8},{18,10},{20,12},{22,14},{24,16},... | collective-permute-start | bytes 393224 | tf_op jit(solution)/shard_map/while/body/eval_jaxpr/ppermute | solution.py:21
  296.7 1.4 collective-permute-start.1
  298.2 8.4 %collective-permute-start.2 = (bf16[32,4096]{1,0:T(8,128)(2,1)S(1)}, bf16[32,4096]{1,0:T(8,128)(2,1)S(1)}, u32[]{:S(2)}, u32[]{:S(2)}) collective-permute-start(bf16[32,4096]{1,0:T(8,128)(2,1)S(1)} %maximum_select_fusion.13), channel_id=1, source_target_pairs={{0,4},{2,6},{4,0},{6,2},{8,12},{10,14},{12,8},{14,10},{16,20},{18,... | collective-permute-start | bytes 786440 | tf_op jit(solution)/shard_map/while/body/eval_jaxpr/ppermute | solution.py:15
  362.9 72.6 %reduce-scatter.2.cloned.1.call-start = ((), (), s32[]{:S(2)}) async-start(), calls=%async_computation.2 | async-start | bytes 786432 | tf_op jit(solution)/shard_map/while/body/eval_jaxpr/reduce_scatter | solution.py:92
  363.0 7.3 %collective-permute-start = (bf16[32,2048]{1,0:T(8,128)(2,1)S(1)}, bf16[32,2048]{1,0:T(8,128)(2,1)S(1)}, u32[]{:S(2)}, u32[]{:S(2)}) collective-permute-start(bf16[32,2048]{1,0:T(8,128)(2,1)S(1)} %broadcast_select_fusion.2), channel_id=1, source_target_pairs={{8,0},{10,2},{12,4},{14,6},{16,8},{18,10},{20,12},{22,14},{24,16},... | collective-permute-start | bytes 393224 | tf_op jit(solution)/shard_map/while/body/eval_jaxpr/ppermute | solution.py:21
  370.4 1.4 collective-permute-start.1
  371.9 8.4 %collective-permute-start.2 = (bf16[32,4096]{1,0:T(8,128)(2,1)S(1)}, bf16[32,4096]{1,0:T(8,128)(2,1)S(1)}, u32[]{:S(2)}, u32[]{:S(2)}) collective-permute-start(bf16[32,4096]{1,0:T(8,128)(2,1)S(1)} %maximum_select_fusion.13), channel_id=1, source_target_pairs={{0,4},{2,6},{4,0},{6,2},{8,12},{10,14},{12,8},{14,10},{16,20},{18,... | collective-permute-start | bytes 786440 | tf_op jit(solution)/shard_map/while/body/eval_jaxpr/ppermute | solution.py:15
  436.6 0.7 copy-start.1
  436.6 0.7 copy-start.4
Sparse Core Ops, SparseCore 0:
  107.5 14.0 reduce-scatter.1
  181.4 10.9 reduce-scatter.1
  255.0 10.9 reduce-scatter.1
  328.7 10.9 reduce-scatter.1
  402.4 10.9 reduce-scatter.1
where the time goes:
time: 445 us; the launch traced here: 444 us
  blocking collectives  199 us (45%)
  waiting for transfers between devices  123 us (28%)
  matrix products  76.6 us (17%)
  other arithmetic  17.1 us (4%)
  between operations  13.8 us (3%)
  starting transfers between devices  12.5 us (3%)
    psum x5, blocking collectives, advance(): totals = totals + lax.psum(increment, 'section')  148 us
    ppermute x12, waiting for transfers between devices, from_partner(): return lax.ppermute(value, axis, pairs)  93.7 us
    dot_general x5, matrix products, advance(): lax.dot_general(by_group, weights, (((1,), (1,)), ((), ())), preferred_el...  58.9 us
    all_to_all x5, blocking collectives, advance(): lax.all_to_all(gate_full, 'dp', split_axis=1, concat_axis=0, tiled=True)  50.8 us
    ppermute x5, waiting for transfers between devices, from_behind(): lax.ppermute(value, axis, [(source, source + steps) for source in range(f...  28.9 us
    dot_general x5, matrix products, score_terms(): jnp.dot(gate_full, right_full, preferred_element_type=jnp.float32)  14.9 us
  transfers between devices with their start and end apart: 22, of which 17 were waited for; matrix products, arithmetic and copies ran while one was open for 5% of the time, Pallas kernels for 0%

commit v1 on v0

--- a/solution.py
+++ b/solution.py
@@ -102,7 +102,7 @@
         updated = lax.dynamic_update_slice_in_dim(grad_store, in_grad, row_start, 0)
         grad_store = jnp.where(in_range, updated, grad_store)
         increment = jnp.where(in_range, increment, 0.0)
-        totals = totals + lax.psum(increment, "section")
+        totals = totals + jnp.sum(lax.all_gather(increment, "section"), axis=0)
         return (in_grad, grad_store, totals)
 
     initial = (

time: 445 us -> 391 us (0.88)
  blocking collectives: 199 us -> 143 us
    psum x5 -> x0, blocking collectives: 148 us -> none  [advance(): totals = totals + lax.psum(increment, 'section')]
    all_gather x0 -> x5, blocking collectives: none -> 92.3 us  [advance(): totals = totals + jnp.sum(lax.all_gather(increment, 'section'), axis=0)]
where the time goes in v1:
time: 391 us; the launch traced here: 390 us
  blocking collectives  143 us (37%)
  waiting for transfers between devices  121 us (31%)
  matrix products  76.6 us (20%)
  other arithmetic  17.3 us (4%)
  starting transfers between devices  16.2 us (4%)
  between operations  13.8 us (4%)
    all_gather x5, blocking collectives, advance(): totals = totals + jnp.sum(lax.all_gather(increment, 'section'), axis=0)  92.3 us
    ppermute x12, waiting for transfers between devices, from_partner(): return lax.ppermute(value, axis, pairs)  90.1 us
    dot_general x5, matrix products, advance(): lax.dot_general(by_group, weights, (((1,), (1,)), ((), ())), preferred_el...  58.9 us
    all_to_all x5, blocking collectives, advance(): lax.all_to_all(gate_full, 'dp', split_axis=1, concat_axis=0, tiled=True)  50.8 us
    ppermute x5, waiting for transfers between devices, from_behind(): lax.ppermute(value, axis, [(source, source + steps) for source in range(f...  30.8 us
    dot_general x5, matrix products, score_terms(): jnp.dot(gate_full, right_full, preferred_element_type=jnp.float32)  14.9 us
    ppermute x12, starting transfers between devices, from_partner(): return lax.ppermute(value, axis, pairs)  9.51 us
    select_n x2, other arithmetic, per_device(): jnp.where(upper_half == 1, jnp.concatenate([partner, right_full], 0), jnp...  8.88 us
  transfers between devices with their start and end apart: 22, of which 17 were waited for; matrix products, arithmetic and copies ran while one was open for 5% of the time, Pallas kernels for 0%

profile of v1, /device:TPU:0, one launch (start us, length us, event | category | flops | bytes accessed | tf_op | source)
XLA Modules:
  0.0 390.2 jit_solution(15185592698765206461)
XLA Ops:
  10.2 3.4 maximum_select_fusion.6
  17.8 44.9 %collective-permute-done.4 = bf16[4096,256]{1,0:T(8,128)(2,1)} collective-permute-done((bf16[4096,256]{1,0:T(8,128)(2,1)}, bf16[4096,256]{1,0:T(8,128)(2,1)}, u32[]{:S(2)}, u32[]{:S(2)}) %collective-permute-start.4) | collective-permute-done | bytes 2097184 | tf_op jit(solution)/shard_map/ppermute | solution.py:15
  62.7 5.5 %maximum_select_fusion.5 = bf16[8192,256]{1,0:T(8,128)(2,1)} fusion(bf16[4096,256]{1,0:T(8,128)(2,1)} %maximum_select_fusion.6, bf16[4096,256]{1,0:T(8,128)(2,1)} %collective-permute-done.4, pred[]{:T(512)} %eq.87), kind=kLoop, calls=%fused_computation.38 | loop fusion | flops 18874368 | bytes 8388609 | tf_op jit(solution)/shard_map/jit(_where)/select_n | solution.py:53
  68.3 314.7 %while.20 = (s32[]{:T(128)}, bf16[32,2048]{1,0:T(8,128)(2,1)S(1)}, bf16[64,2048]{1,0:T(8,128)(2,1)S(1)}, f32[2,16]{1,0:T(2,128)S(1)}, pred[]{:T(512)}, /*index=5...) while((s32[]{:T(128)}, bf16[32,2048]{1,0:T(8,128)(2,1)S(1)}, ...), condition=%wide.region_4.5_spmd.clone, body=%wide.region_0.4_spmd.clone.sunk | while | flops 1248227584 | bytes 33236612 | solution.py:113
  69.7 5.5 %collective-permute-done = bf16[32,2048]{1,0:T(8,128)(2,1)S(1)} collective-permute-done((bf16[32,2048]{1,0:T(8,128)(2,1)S(1)}, bf16[32,2048]{1,0:T(8,128)(2,1)S(1)}, u32[]{:S(2)}, u32[]{:S(2)}) %collective-permute-start) | collective-permute-done | bytes 131104 | tf_op jit(solution)/shard_map/while/body/eval_jaxpr/ppermute | solution.py:21
  78.7 6.5 %collective-permute-done.2 = bf16[32,4096]{1,0:T(8,128)(2,1)S(1)} collective-permute-done((bf16[32,4096]{1,0:T(8,128)(2,1)S(1)}, bf16[32,4096]{1,0:T(8,128)(2,1)S(1)}, u32[]{:S(2)}, u32[]{:S(2)}) %collective-permute-start.2) | collective-permute-done | bytes 262176 | tf_op jit(solution)/shard_map/while/body/eval_jaxpr/ppermute | solution.py:15
  85.3 10.3 %all_to_all.38 = bf16[32,2,4096]{2,0,1:T(8,128)(2,1)S(1)} all-to-all(bf16[32,2,4096]{2,0,1:T(8,128)(2,1)S(1)} %maximum_select_fusion.14), channel_id=1, replica_groups=mesh['section'=16,'dp'=2] {'dp'}, dimensions={1} | all-to-all | bytes 1048576 | tf_op jit(solution)/shard_map/while/body/eval_jaxpr/all_to_all | solution.py:91
  95.6 11.8 %fusion.52 = f32[64,2048]{1,0:T(8,128)} fusion(bf16[64,4096]{1,0:T(8,128)(2,1)S(1)} %bitcast.48, bf16[2048,4096]{1,0:T(8,128)(2,1)} %get-tuple-element.581), kind=kOutput, calls=%fused_computation.50.clone.1 | convolution fusion | flops 1073741824 | bytes 17825792 | tf_op jit(solution)/shard_map/while/body/eval_jaxpr/dot_general | solution.py:93
  107.8 2.9 convolution_multiply_fusion.2
  111.1 19.8 %all-gather.4 = f32[16,2,16]{2,1,0:T(2,128)S(1)} all-gather(f32[1,2,16]{2,1,0:T(2,128)S(1)} %fusion.54), channel_id=2, replica_groups=mesh['section'=16,'dp'=2] {'section'}, dimensions={0}, use_global_device_ids=true | all-gather | bytes 2176 | tf_op jit(solution)/shard_map/while/body/eval_jaxpr/all_gather | solution.py:105
  133.4 6.3 %collective-permute-done = bf16[32,2048]{1,0:T(8,128)(2,1)S(1)} collective-permute-done((bf16[32,2048]{1,0:T(8,128)(2,1)S(1)}, bf16[32,2048]{1,0:T(8,128)(2,1)S(1)}, u32[]{:S(2)}, u32[]{:S(2)}) %collective-permute-start) | collective-permute-done | bytes 131104 | tf_op jit(solution)/shard_map/while/body/eval_jaxpr/ppermute | solution.py:21
  141.5 8.3 %collective-permute-done.2 = bf16[32,4096]{1,0:T(8,128)(2,1)S(1)} collective-permute-done((bf16[32,4096]{1,0:T(8,128)(2,1)S(1)}, bf16[32,4096]{1,0:T(8,128)(2,1)S(1)}, u32[]{:S(2)}, u32[]{:S(2)}) %collective-permute-start.2) | collective-permute-done | bytes 262176 | tf_op jit(solution)/shard_map/while/body/eval_jaxpr/ppermute | solution.py:15
  149.8 10.1 %all_to_all.38 = bf16[32,2,4096]{2,0,1:T(8,128)(2,1)S(1)} all-to-all(bf16[32,2,4096]{2,0,1:T(8,128)(2,1)S(1)} %maximum_select_fusion.14), channel_id=1, replica_groups=mesh['section'=16,'dp'=2] {'dp'}, dimensions={1} | all-to-all | bytes 1048576 | tf_op jit(solution)/shard_map/while/body/eval_jaxpr/all_to_all | solution.py:91
  159.9 11.8 %fusion.52 = f32[64,2048]{1,0:T(8,128)} fusion(bf16[64,4096]{1,0:T(8,128)(2,1)S(1)} %bitcast.48, bf16[2048,4096]{1,0:T(8,128)(2,1)} %get-tuple-element.581), kind=kOutput, calls=%fused_computation.50.clone.1 | convolution fusion | flops 1073741824 | bytes 17825792 | tf_op jit(solution)/shard_map/while/body/eval_jaxpr/dot_general | solution.py:93
  172.1 3.0 convolution_multiply_fusion.2
  175.5 17.6 %all-gather.4 = f32[16,2,16]{2,1,0:T(2,128)S(1)} all-gather(f32[1,2,16]{2,1,0:T(2,128)S(1)} %fusion.54), channel_id=2, replica_groups=mesh['section'=16,'dp'=2] {'section'}, dimensions={0}, use_global_device_ids=true | all-gather | bytes 2176 | tf_op jit(solution)/shard_map/while/body/eval_jaxpr/all_gather | solution.py:105
  195.6 6.3 %collective-permute-done = bf16[32,2048]{1,0:T(8,128)(2,1)S(1)} collective-permute-done((bf16[32,2048]{1,0:T(8,128)(2,1)S(1)}, bf16[32,2048]{1,0:T(8,128)(2,1)S(1)}, u32[]{:S(2)}, u32[]{:S(2)}) %collective-permute-start) | collective-permute-done | bytes 131104 | tf_op jit(solution)/shard_map/while/body/eval_jaxpr/ppermute | solution.py:21
  205.2 6.7 %collective-permute-done.2 = bf16[32,4096]{1,0:T(8,128)(2,1)S(1)} collective-permute-done((bf16[32,4096]{1,0:T(8,128)(2,1)S(1)}, bf16[32,4096]{1,0:T(8,128)(2,1)S(1)}, u32[]{:S(2)}, u32[]{:S(2)}) %collective-permute-start.2) | collective-permute-done | bytes 262176 | tf_op jit(solution)/shard_map/while/body/eval_jaxpr/ppermute | solution.py:15
  212.1 10.1 %all_to_all.38 = bf16[32,2,4096]{2,0,1:T(8,128)(2,1)S(1)} all-to-all(bf16[32,2,4096]{2,0,1:T(8,128)(2,1)S(1)} %maximum_select_fusion.14), channel_id=1, replica_groups=mesh['section'=16,'dp'=2] {'dp'}, dimensions={1} | all-to-all | bytes 1048576 | tf_op jit(solution)/shard_map/while/body/eval_jaxpr/all_to_all | solution.py:91
  222.2 11.8 %fusion.52 = f32[64,2048]{1,0:T(8,128)} fusion(bf16[64,4096]{1,0:T(8,128)(2,1)S(1)} %bitcast.48, bf16[2048,4096]{1,0:T(8,128)(2,1)} %get-tuple-element.581), kind=kOutput, calls=%fused_computation.50.clone.1 | convolution fusion | flops 1073741824 | bytes 17825792 | tf_op jit(solution)/shard_map/while/body/eval_jaxpr/dot_general | solution.py:93
  237.7 18.7 %all-gather.4 = f32[16,2,16]{2,1,0:T(2,128)S(1)} all-gather(f32[1,2,16]{2,1,0:T(2,128)S(1)} %fusion.54), channel_id=2, replica_groups=mesh['section'=16,'dp'=2] {'section'}, dimensions={0}, use_global_device_ids=true | all-gather | bytes 2176 | tf_op jit(solution)/shard_map/while/body/eval_jaxpr/all_gather | solution.py:105
  258.8 6.3 %collective-permute-done = bf16[32,2048]{1,0:T(8,128)(2,1)S(1)} collective-permute-done((bf16[32,2048]{1,0:T(8,128)(2,1)S(1)}, bf16[32,2048]{1,0:T(8,128)(2,1)S(1)}, u32[]{:S(2)}, u32[]{:S(2)}) %collective-permute-start) | collective-permute-done | bytes 131104 | tf_op jit(solution)/shard_map/while/body/eval_jaxpr/ppermute | solution.py:21
  267.4 7.8 %collective-permute-done.2 = bf16[32,4096]{1,0:T(8,128)(2,1)S(1)} collective-permute-done((bf16[32,4096]{1,0:T(8,128)(2,1)S(1)}, bf16[32,4096]{1,0:T(8,128)(2,1)S(1)}, u32[]{:S(2)}, u32[]{:S(2)}) %collective-permute-start.2) | collective-permute-done | bytes 262176 | tf_op jit(solution)/shard_map/while/body/eval_jaxpr/ppermute | solution.py:15
  275.3 10.1 %all_to_all.38 = bf16[32,2,4096]{2,0,1:T(8,128)(2,1)S(1)} all-to-all(bf16[32,2,4096]{2,0,1:T(8,128)(2,1)S(1)} %maximum_select_fusion.14), channel_id=1, replica_groups=mesh['section'=16,'dp'=2] {'dp'}, dimensions={1} | all-to-all | bytes 1048576 | tf_op jit(solution)/shard_map/while/body/eval_jaxpr/all_to_all | solution.py:91
  285.4 11.8 %fusion.52 = f32[64,2048]{1,0:T(8,128)} fusion(bf16[64,4096]{1,0:T(8,128)(2,1)S(1)} %bitcast.48, bf16[2048,4096]{1,0:T(8,128)(2,1)} %get-tuple-element.581), kind=kOutput, calls=%fused_computation.50.clone.1 | convolution fusion | flops 1073741824 | bytes 17825792 | tf_op jit(solution)/shard_map/while/body/eval_jaxpr/dot_general | solution.py:93
  297.6 3.0 convolution_multiply_fusion.2
  301.0 17.5 %all-gather.4 = f32[16,2,16]{2,1,0:T(2,128)S(1)} all-gather(f32[1,2,16]{2,1,0:T(2,128)S(1)} %fusion.54), channel_id=2, replica_groups=mesh['section'=16,'dp'=2] {'section'}, dimensions={0}, use_global_device_ids=true | all-gather | bytes 2176 | tf_op jit(solution)/shard_map/while/body/eval_jaxpr/all_gather | solution.py:105
  321.0 6.3 %collective-permute-done = bf16[32,2048]{1,0:T(8,128)(2,1)S(1)} collective-permute-done((bf16[32,2048]{1,0:T(8,128)(2,1)S(1)}, bf16[32,2048]{1,0:T(8,128)(2,1)S(1)}, u32[]{:S(2)}, u32[]{:S(2)}) %collective-permute-start) | collective-permute-done | bytes 131104 | tf_op jit(solution)/shard_map/while/body/eval_jaxpr/ppermute | solution.py:21
  330.7 6.6 %collective-permute-done.2 = bf16[32,4096]{1,0:T(8,128)(2,1)S(1)} collective-permute-done((bf16[32,4096]{1,0:T(8,128)(2,1)S(1)}, bf16[32,4096]{1,0:T(8,128)(2,1)S(1)}, u32[]{:S(2)}, u32[]{:S(2)}) %collective-permute-start.2) | collective-permute-done | bytes 262176 | tf_op jit(solution)/shard_map/while/body/eval_jaxpr/ppermute | solution.py:15
  337.5 10.1 %all_to_all.38 = bf16[32,2,4096]{2,0,1:T(8,128)(2,1)S(1)} all-to-all(bf16[32,2,4096]{2,0,1:T(8,128)(2,1)S(1)} %maximum_select_fusion.14), channel_id=1, replica_groups=mesh['section'=16,'dp'=2] {'dp'}, dimensions={1} | all-to-all | bytes 1048576 | tf_op jit(solution)/shard_map/while/body/eval_jaxpr/all_to_all | solution.py:91
  347.6 11.8 %fusion.52 = f32[64,2048]{1,0:T(8,128)} fusion(bf16[64,4096]{1,0:T(8,128)(2,1)S(1)} %bitcast.48, bf16[2048,4096]{1,0:T(8,128)(2,1)} %get-tuple-element.581), kind=kOutput, calls=%fused_computation.50.clone.1 | convolution fusion | flops 1073741824 | bytes 17825792 | tf_op jit(solution)/shard_map/while/body/eval_jaxpr/dot_general | solution.py:93
  363.1 18.8 %all-gather.4 = f32[16,2,16]{2,1,0:T(2,128)S(1)} all-gather(f32[1,2,16]{2,1,0:T(2,128)S(1)} %fusion.54), channel_id=2, replica_groups=mesh['section'=16,'dp'=2] {'section'}, dimensions={0}, use_global_device_ids=true | all-gather | bytes 2176 | tf_op jit(solution)/shard_map/while/body/eval_jaxpr/all_gather | solution.py:105
  (130 shorter events, 44.2 us)
Async XLA Ops:
  7.2 9.3 %copy-start.5 = (s32[2]{0:T(128)S(1)}, s32[2]{0:T(128)}, u32[]{:S(2)}) copy-start(s32[2]{0:T(128)} %param.11) | copy-start | bytes 28
  7.2 9.3 %copy-start.6 = (s32[64]{0:T(128)S(1)}, s32[64]{0:T(128)}, u32[]{:S(2)}) copy-start(s32[64]{0:T(128)} %param.12) | copy-start | bytes 772
  7.2 3.1 collective-permute-start.3
  13.6 49.1 %collective-permute-start.4 = (bf16[4096,256]{1,0:T(8,128)(2,1)}, bf16[4096,256]{1,0:T(8,128)(2,1)}, u32[]{:S(2)}, u32[]{:S(2)}) collective-permute-start(bf16[4096,256]{1,0:T(8,128)(2,1)} %maximum_select_fusion.6), channel_id=1, source_target_pairs={{0,4},{2,6},{4,0},{6,2},{8,12},{10,14},{12,8},{14,10},{16,20},{18,... | collective-permute-start | bytes 6291464 | tf_op jit(solution)/shard_map/ppermute | solution.py:15
  17.8 50.5 %copy-start = (bf16[2048,256]{1,0:T(8,128)(2,1)S(1)}, bf16[2048,256]{1,0:T(8,128)(2,1)}, u32[]{:S(2)}) copy-start(bf16[2048,256]{1,0:T(8,128)(2,1)} %param.16) | copy-start | bytes 3145732
  17.8 50.5 %copy-start.2 = (bf16[64,2048]{1,0:T(8,128)(2,1)S(1)}, bf16[64,2048]{1,0:T(8,128)(2,1)}, u32[]{:S(2)}) copy-start(bf16[64,2048]{1,0:T(8,128)(2,1)} %param.13) | copy-start | bytes 786436
  17.8 50.5 %copy-start.3 = (bf16[64,2048]{1,0:T(8,128)(2,1)S(1)}, bf16[64,2048]{1,0:T(8,128)(2,1)}, u32[]{:S(2)}) copy-start(bf16[64,2048]{1,0:T(8,128)(2,1)} %param.14) | copy-start | bytes 786436
  68.3 62.6 %reduce-scatter.2.cloned.1.call-start = ((), (), s32[]{:S(2)}) async-start(), calls=%async_computation.2 | async-start | bytes 786432 | tf_op jit(solution)/shard_map/while/body/eval_jaxpr/reduce_scatter | solution.py:92
  68.4 6.9 %collective-permute-start = (bf16[32,2048]{1,0:T(8,128)(2,1)S(1)}, bf16[32,2048]{1,0:T(8,128)(2,1)S(1)}, u32[]{:S(2)}, u32[]{:S(2)}) collective-permute-start(bf16[32,2048]{1,0:T(8,128)(2,1)S(1)} %broadcast_select_fusion.2), channel_id=1, source_target_pairs={{8,0},{10,2},{12,4},{14,6},{16,8},{18,10},{20,12},{22,14},{24,16},... | collective-permute-start | bytes 393224 | tf_op jit(solution)/shard_map/while/body/eval_jaxpr/ppermute | solution.py:21
  75.3 1.4 collective-permute-start.1
  76.8 8.4 %collective-permute-start.2 = (bf16[32,4096]{1,0:T(8,128)(2,1)S(1)}, bf16[32,4096]{1,0:T(8,128)(2,1)S(1)}, u32[]{:S(2)}, u32[]{:S(2)}) collective-permute-start(bf16[32,4096]{1,0:T(8,128)(2,1)S(1)} %maximum_select_fusion.13), channel_id=1, source_target_pairs={{0,4},{2,6},{4,0},{6,2},{8,12},{10,14},{12,8},{14,10},{16,20},{18,... | collective-permute-start | bytes 786440 | tf_op jit(solution)/shard_map/while/body/eval_jaxpr/ppermute | solution.py:15
  132.0 61.2 %reduce-scatter.2.cloned.1.call-start = ((), (), s32[]{:S(2)}) async-start(), calls=%async_computation.2 | async-start | bytes 786432 | tf_op jit(solution)/shard_map/while/body/eval_jaxpr/reduce_scatter | solution.py:92
  132.1 7.6 %collective-permute-start = (bf16[32,2048]{1,0:T(8,128)(2,1)S(1)}, bf16[32,2048]{1,0:T(8,128)(2,1)S(1)}, u32[]{:S(2)}, u32[]{:S(2)}) collective-permute-start(bf16[32,2048]{1,0:T(8,128)(2,1)S(1)} %broadcast_select_fusion.2), channel_id=1, source_target_pairs={{8,0},{10,2},{12,4},{14,6},{16,8},{18,10},{20,12},{22,14},{24,16},... | collective-permute-start | bytes 393224 | tf_op jit(solution)/shard_map/while/body/eval_jaxpr/ppermute | solution.py:21
  139.8 1.4 collective-permute-start.1
  141.3 8.4 %collective-permute-start.2 = (bf16[32,4096]{1,0:T(8,128)(2,1)S(1)}, bf16[32,4096]{1,0:T(8,128)(2,1)S(1)}, u32[]{:S(2)}, u32[]{:S(2)}) collective-permute-start(bf16[32,4096]{1,0:T(8,128)(2,1)S(1)} %maximum_select_fusion.13), channel_id=1, source_target_pairs={{0,4},{2,6},{4,0},{6,2},{8,12},{10,14},{12,8},{14,10},{16,20},{18,... | collective-permute-start | bytes 786440 | tf_op jit(solution)/shard_map/while/body/eval_jaxpr/ppermute | solution.py:15
  194.2 62.2 %reduce-scatter.2.cloned.1.call-start = ((), (), s32[]{:S(2)}) async-start(), calls=%async_computation.2 | async-start | bytes 786432 | tf_op jit(solution)/shard_map/while/body/eval_jaxpr/reduce_scatter | solution.py:92
  194.3 7.6 %collective-permute-start = (bf16[32,2048]{1,0:T(8,128)(2,1)S(1)}, bf16[32,2048]{1,0:T(8,128)(2,1)S(1)}, u32[]{:S(2)}, u32[]{:S(2)}) collective-permute-start(bf16[32,2048]{1,0:T(8,128)(2,1)S(1)} %broadcast_select_fusion.2), channel_id=1, source_target_pairs={{8,0},{10,2},{12,4},{14,6},{16,8},{18,10},{20,12},{22,14},{24,16},... | collective-permute-start | bytes 393224 | tf_op jit(solution)/shard_map/while/body/eval_jaxpr/ppermute | solution.py:21
  202.1 1.4 collective-permute-start.1
  203.6 8.4 %collective-permute-start.2 = (bf16[32,4096]{1,0:T(8,128)(2,1)S(1)}, bf16[32,4096]{1,0:T(8,128)(2,1)S(1)}, u32[]{:S(2)}, u32[]{:S(2)}) collective-permute-start(bf16[32,4096]{1,0:T(8,128)(2,1)S(1)} %maximum_select_fusion.13), channel_id=1, source_target_pairs={{0,4},{2,6},{4,0},{6,2},{8,12},{10,14},{12,8},{14,10},{16,20},{18,... | collective-permute-start | bytes 786440 | tf_op jit(solution)/shard_map/while/body/eval_jaxpr/ppermute | solution.py:15
  257.4 61.1 %reduce-scatter.2.cloned.1.call-start = ((), (), s32[]{:S(2)}) async-start(), calls=%async_computation.2 | async-start | bytes 786432 | tf_op jit(solution)/shard_map/while/body/eval_jaxpr/reduce_scatter | solution.py:92
  257.5 7.6 %collective-permute-start = (bf16[32,2048]{1,0:T(8,128)(2,1)S(1)}, bf16[32,2048]{1,0:T(8,128)(2,1)S(1)}, u32[]{:S(2)}, u32[]{:S(2)}) collective-permute-start(bf16[32,2048]{1,0:T(8,128)(2,1)S(1)} %broadcast_select_fusion.2), channel_id=1, source_target_pairs={{8,0},{10,2},{12,4},{14,6},{16,8},{18,10},{20,12},{22,14},{24,16},... | collective-permute-start | bytes 393224 | tf_op jit(solution)/shard_map/while/body/eval_jaxpr/ppermute | solution.py:21
  265.3 1.4 collective-permute-start.1
  266.8 8.4 %collective-permute-start.2 = (bf16[32,4096]{1,0:T(8,128)(2,1)S(1)}, bf16[32,4096]{1,0:T(8,128)(2,1)S(1)}, u32[]{:S(2)}, u32[]{:S(2)}) collective-permute-start(bf16[32,4096]{1,0:T(8,128)(2,1)S(1)} %maximum_select_fusion.13), channel_id=1, source_target_pairs={{0,4},{2,6},{4,0},{6,2},{8,12},{10,14},{12,8},{14,10},{16,20},{18,... | collective-permute-start | bytes 786440 | tf_op jit(solution)/shard_map/while/body/eval_jaxpr/ppermute | solution.py:15
  319.6 62.3 %reduce-scatter.2.cloned.1.call-start = ((), (), s32[]{:S(2)}) async-start(), calls=%async_computation.2 | async-start | bytes 786432 | tf_op jit(solution)/shard_map/while/body/eval_jaxpr/reduce_scatter | solution.py:92
  319.7 7.6 %collective-permute-start = (bf16[32,2048]{1,0:T(8,128)(2,1)S(1)}, bf16[32,2048]{1,0:T(8,128)(2,1)S(1)}, u32[]{:S(2)}, u32[]{:S(2)}) collective-permute-start(bf16[32,2048]{1,0:T(8,128)(2,1)S(1)} %broadcast_select_fusion.2), channel_id=1, source_target_pairs={{8,0},{10,2},{12,4},{14,6},{16,8},{18,10},{20,12},{22,14},{24,16},... | collective-permute-start | bytes 393224 | tf_op jit(solution)/shard_map/while/body/eval_jaxpr/ppermute | solution.py:21
  327.5 1.4 collective-permute-start.1
  329.0 8.4 %collective-permute-start.2 = (bf16[32,4096]{1,0:T(8,128)(2,1)S(1)}, bf16[32,4096]{1,0:T(8,128)(2,1)S(1)}, u32[]{:S(2)}, u32[]{:S(2)}) collective-permute-start(bf16[32,4096]{1,0:T(8,128)(2,1)S(1)} %maximum_select_fusion.13), channel_id=1, source_target_pairs={{0,4},{2,6},{4,0},{6,2},{8,12},{10,14},{12,8},{14,10},{16,20},{18,... | collective-permute-start | bytes 786440 | tf_op jit(solution)/shard_map/while/body/eval_jaxpr/ppermute | solution.py:15
  383.0 0.7 copy-start.1
  383.0 0.7 copy-start.4
Sparse Core Ops, SparseCore 0:
  107.5 14.0 reduce-scatter.1
  171.9 10.9 reduce-scatter.1
  234.1 11.9 reduce-scatter.1
  297.3 10.8 reduce-scatter.1
  359.5 12.0 reduce-scatter.1
